TPU v7x, 512 devices: a whole 4x8x8 slice. The times are simulated.
512 devices in a mesh: gx: 8 (over x, z_lo), gy: 4 (over z_hi), gz: 16 (over y, core).
Axes of the slice: x: 4, y: 8, z: 8 (z_hi: 4, z_lo: 2; z = z_hi * 2 + z_lo), core: 2. Of those that a mesh axis runs over, the one named last changes fastest.
Arguments:
- density: float32 [768, 1024, 512], P('gz', 'gx', 'gy'), may hold values from 0.0005 to 0.01
- shear_offsets: int32 [2, 768], P(None, 'gz'), may hold values from 0 to 192, as said below
- shear_fractions: float32 [2, 768], P(None, 'gz'), may hold values from 0 to 1
- flat_field: float32 [1024, 512], P(('gx', 'gz'), 'gy'), may hold values from 0.5 to 1.5
Outputs:
- normalized: float32 [1024, 512], P(('gx', 'gz'), 'gy')
Inputs may be any that keep to these rules, and one draw needn't show every extreme that they name: `shear_offsets`: in each row, the shift never falls from one slice to the next and rises by at most 1; it is 0 or 1 at slice 0 and exactly 192 at the last slice.
All inputs are finite; a program needn't handle non-finite values.
Results may differ from a plain program's by a relative error of at most 0.0003.
Values sent between devices are 32-bit elements; how exact they have to be, the bound alone decides.
A program may use at most 64 MiB of HBM per device.

v0:
```python
import functools

import jax
import jax.numpy as jnp
from jax import lax
from jax.sharding import Mesh
from jax.sharding import PartitionSpec as P

GZ = ("gz_0", "gz_1")
GX = ("gx_0", "gx_1")
GX_GY_GZ = ("gx_0", "gx_1", "gy", "gz_0", "gz_1")
GX_GZ = ("gx_0", "gx_1", "gz_0", "gz_1")


def passed_along(value, axis, steps):
    count = lax.axis_size(axis)
    initial, last = (max(0, -steps), min(count, count - steps))
    return lax.ppermute(value, axis, [(source, source + steps) for source in range(initial, last)])


def in_blocks(array, dim, size):
    before, after = (array.shape[:dim], array.shape[dim + 1 :])
    return jnp.moveaxis(array.reshape(*before, size, -1, *after), dim, 0)


def sum_at_owner(array, axis, dim):
    size = lax.axis_size(axis)
    tiles = lax.all_to_all(in_blocks(array, dim, size), axis, 0, 0, tiled=True)
    return jnp.sum(tiles, axis=0)


def one_axis_at_a_time(array, axes):
    return functools.reduce(lax.pmax, axes, array)


def shards(density, shear_offsets, shear_fractions, flat_field):
    slices, tile_rows, tile_cols = density.shape
    center = slices * lax.axis_size(GZ) // 8
    margin = center + 1
    used_cols = tile_cols + 2 * margin
    padded_cols = (used_cols + 127) // 128 * 128
    screen = jnp.zeros((tile_rows + 2 * margin, padded_cols), jnp.float32)
    source_cols = lax.broadcasted_iota(jnp.int32, (tile_cols, padded_cols), 0)
    target_cols = lax.broadcasted_iota(jnp.int32, (tile_cols, padded_cols), 1)

    def march_slab(slice_index, carry):
        slab = lax.dynamic_index_in_dim(density, slice_index, 0, keepdims=False)
        offset_pair = lax.dynamic_index_in_dim(shear_offsets, slice_index, 1, keepdims=False)
        frac_pair = lax.dynamic_index_in_dim(shear_fractions, slice_index, 1, keepdims=False)
        start_u = offset_pair[0] - center + margin
        start_v = offset_pair[1] - center + margin
        frac_u = frac_pair[0]
        frac_v = frac_pair[1]
        placed = source_cols + start_v
        placing = jnp.where(target_cols == placed, 1.0 - frac_v, 0.0) + jnp.where(
            target_cols == placed + 1, frac_v, 0.0
        )
        spread_cols = jnp.dot(
            slab, placing, precision=lax.Precision.HIGHEST, preferred_element_type=jnp.float32
        )
        spread = jnp.pad(spread_cols * (1.0 - frac_u), ((0, 1), (0, 0)))
        spread = spread + jnp.pad(spread_cols * frac_u, ((1, 0), (0, 0)))
        window = lax.dynamic_slice(carry, (start_u, jnp.int32(0)), (tile_rows + 1, padded_cols))
        return lax.dynamic_update_slice(carry, window + spread, (start_u, jnp.int32(0)))

    screen = lax.fori_loop(0, slices, march_slab, screen)
    screen = screen[:, :used_cols]
    band = screen[margin : margin + tile_rows]
    from_lower = passed_along(screen[margin + tile_rows :], GX, 1)
    from_upper = passed_along(screen[:margin], GX, -1)
    band = band.at[:margin].add(from_lower)
    band = band.at[tile_rows - margin :].add(from_upper)
    tile_total = band[:, margin : margin + tile_cols]
    from_left = passed_along(band[:, margin + tile_cols :], "gy", 1)
    from_right = passed_along(band[:, :margin], "gy", -1)
    tile_total = tile_total.at[:, :margin].add(from_left)
    tile_total = tile_total.at[:, tile_cols - margin :].add(from_right)
    integral = sum_at_owner(tile_total, GZ, 0)
    detected = flat_field * jnp.exp(-integral)
    largest = one_axis_at_a_time(jnp.max(detected), GX_GY_GZ)
    return detected / largest


def solution(mesh):
    split = Mesh(
        mesh.devices.reshape(4, 2, mesh.shape["gy"], 8, 2), ("gx_0", "gx_1", "gy", "gz_0", "gz_1")
    )
    return jax.shard_map(
        shards,
        mesh=split,
        in_specs=(P(GZ, GX, "gy"), P(None, GZ), P(None, GZ), P(GX_GZ, "gy")),
        out_specs=P(GX_GZ, "gy"),
        check_vma=False,
    )
```

profile of v0, /device:TPU:1, one launch (start us, length us, event | category | flops | bytes accessed | tf_op | source)
XLA Modules:
  0.0 578.8 jit_solution(16294964130230961524)
XLA Ops:
  0.0 482.5 %while.24 = (s32[]{:T(128)}, f32[322,384]{1,0:T(8,128)S(1)}, s32[2,48]{1,0:T(2,128)}, f32[48,128,128]{2,1,0:T(8,128)}, f32[2,48]{1,0:T(2,128)}, /*index=5*/s32[]...) while((s32[]{:T(128)}, f32[322,384]{1,0:T(8,128)S(1)}, ...), condition=%wide.region_1.2_spmd.clone.clone, body=%wide.region_0.1_spmd.clone.clone.sunk | while | flops 76038912 | bytes 1646863 | solution.py:66
  4.7 2.5 broadcast_multiply_fusion.3
  14.7 2.5 broadcast_multiply_fusion.3
  24.8 2.5 broadcast_multiply_fusion.3
  34.8 2.5 broadcast_multiply_fusion.3
  38.7 1.5 dynamic_update_slice.17
  44.9 2.5 broadcast_multiply_fusion.3
  54.9 2.5 broadcast_multiply_fusion.3
  65.0 2.5 broadcast_multiply_fusion.3
  75.0 2.5 broadcast_multiply_fusion.3
  85.1 2.5 broadcast_multiply_fusion.3
  95.1 2.5 broadcast_multiply_fusion.3
  105.2 2.5 broadcast_multiply_fusion.3
  115.2 2.5 broadcast_multiply_fusion.3
  125.3 2.5 broadcast_multiply_fusion.3
  135.3 2.5 broadcast_multiply_fusion.3
  145.4 2.5 broadcast_multiply_fusion.3
  155.4 2.5 broadcast_multiply_fusion.3
  165.5 2.5 broadcast_multiply_fusion.3
  175.5 2.5 broadcast_multiply_fusion.3
  179.4 1.5 dynamic_update_slice.17
  185.6 2.5 broadcast_multiply_fusion.3
  195.6 2.5 broadcast_multiply_fusion.3
  205.7 2.5 broadcast_multiply_fusion.3
  215.7 2.5 broadcast_multiply_fusion.3
  225.8 2.5 broadcast_multiply_fusion.3
  229.7 1.5 dynamic_update_slice.17
  235.8 2.5 broadcast_multiply_fusion.3
  239.8 1.5 dynamic_update_slice.17
  245.9 2.5 broadcast_multiply_fusion.3
  256.0 2.5 broadcast_multiply_fusion.3
  266.0 2.5 broadcast_multiply_fusion.3
  276.1 2.5 broadcast_multiply_fusion.3
  286.1 2.5 broadcast_multiply_fusion.3
  296.2 2.5 broadcast_multiply_fusion.3
  306.2 2.5 broadcast_multiply_fusion.3
  316.3 2.5 broadcast_multiply_fusion.3
  326.3 2.5 broadcast_multiply_fusion.3
  336.4 2.5 broadcast_multiply_fusion.3
  346.4 2.5 broadcast_multiply_fusion.3
  356.5 2.5 broadcast_multiply_fusion.3
  366.5 2.5 broadcast_multiply_fusion.3
  376.6 2.5 broadcast_multiply_fusion.3
  386.6 2.5 broadcast_multiply_fusion.3
  396.7 2.5 broadcast_multiply_fusion.3
  406.7 2.5 broadcast_multiply_fusion.3
  416.8 2.5 broadcast_multiply_fusion.3
  426.8 2.5 broadcast_multiply_fusion.3
  436.9 2.5 broadcast_multiply_fusion.3
  446.9 2.5 broadcast_multiply_fusion.3
  457.0 2.5 broadcast_multiply_fusion.3
  467.0 2.5 broadcast_multiply_fusion.3
  477.1 2.5 broadcast_multiply_fusion.3
  482.6 4.8 collective-permute-start
  487.4 2.2 collective-permute-done
  491.8 4.3 collective-permute-done.1
  496.9 6.7 %collective-permute-start.2 = (f32[128,97]{1,0:T(8,128)S(1)}, f32[128,97]{1,0:T(8,128)S(1)}, u32[]{:S(2)}, u32[]{:S(2)}) collective-permute-start(f32[128,97]{1,0:T(8,128)S(1)} %get-tuple-element.367), channel_id=1, source_target_pairs={{0,16},{16,32},{32,48},{1,17},{17,33},{33,49},{2,18},{18,34},{34,5... | collective-permute-start | bytes 149000 | tf_op jit(solution)/shard_map/ppermute | solution.py:18
  506.8 5.3 collective-permute-done.3
  512.7 14.1 %all_to_all.5 = f32[16,8,128]{2,1,0:T(8,128)S(1)} all-to-all(f32[16,8,128]{2,1,0:T(8,128)S(1)} %bitcast.23), channel_id=1, replica_groups=mesh['gx_0'=4,'gx_1'=2,'gy'=4,'gz_0'=8,'gz_1'=2] {'gz_0','gz_1'}, dimensions={0} | all-to-all | bytes 131072 | tf_op jit(solution)/shard_map/all_to_all | solution.py:28
  527.5 10.8 %pmax.35 = f32[]{:T(128)} all-reduce(f32[]{:T(128)} %fusion.19), channel_id=1, replica_groups=mesh['gx_0'=4,'gx_1'=2,'gy'=4,'gz_0'=8,'gz_1'=2] {'gx_0'}, use_global_device_ids=true, to_apply=%region_5.6 | all-reduce | flops 1 | bytes 8 | tf_op jit(solution)/shard_map/pmax | solution.py:33
  538.3 4.4 pmax.36
  542.7 11.3 %pmax.37 = f32[]{:T(128)} all-reduce(f32[]{:T(128)} %pmax.36), channel_id=1, replica_groups=mesh['gx_0'=4,'gx_1'=2,'gy'=4,'gz_0'=8,'gz_1'=2] {'gy'}, use_global_device_ids=true, to_apply=%region_7.8 | all-reduce | flops 1 | bytes 8 | tf_op jit(solution)/shard_map/pmax | solution.py:33
  554.0 11.7 %pmax.38 = f32[]{:T(128)} all-reduce(f32[]{:T(128)} %pmax.37), channel_id=1, replica_groups=mesh['gx_0'=4,'gx_1'=2,'gy'=4,'gz_0'=8,'gz_1'=2] {'gz_0'}, use_global_device_ids=true, to_apply=%region_8.9 | all-reduce | flops 1 | bytes 8 | tf_op jit(solution)/shard_map/pmax | solution.py:33
  565.7 11.8 %pmax.39 = f32[]{:T(128)} all-reduce(f32[]{:T(128)} %pmax.38), channel_id=1, replica_groups=mesh['gx_0'=4,'gx_1'=2,'gy'=4,'gz_0'=8,'gz_1'=2] {'gz_1'}, use_global_device_ids=true, to_apply=%region_9.10 | all-reduce | flops 1 | bytes 8 | tf_op jit(solution)/shard_map/pmax | solution.py:33
  (306 shorter events, 207.4 us)
Async XLA Ops:
  482.5 44.3 %copy-start = (f32[8,128]{1,0:T(8,128)S(1)}, f32[8,128]{1,0:T(8,128)}, u32[]{:S(2)}) copy-start(f32[8,128]{1,0:T(8,128)} %param.17) | copy-start | bytes 12292
  482.6 7.0 %collective-permute-start = (f32[97,322]{1,0:T(8,128)S(1)}, f32[97,322]{1,0:T(8,128)S(1)}, u32[]{:S(2)}, u32[]{:S(2)}) collective-permute-start(f32[97,322]{1,0:T(8,128)S(1)} %slice.162), channel_id=1, source_target_pairs={{0,64},{64,128},{128,192},{192,256},{256,320},{320,384},{384,448},... | collective-permute-start | bytes 374816 | tf_op jit(solution)/shard_map/ppermute | solution.py:18
  489.6 6.5 %collective-permute-start.1 = (f32[97,322]{1,0:T(8,128)S(1)}, f32[97,322]{1,0:T(8,128)S(1)}, u32[]{:S(2)}, u32[]{:S(2)}) collective-permute-start(f32[97,322]{1,0:T(8,128)S(1)} %get-tuple-element.364), channel_id=1, source_target_pairs={{64,0},{128,64},{192,128},{256,192},{320,256},{384,320},{448,384},... | collective-permute-start | bytes 374816 | tf_op jit(solution)/shard_map/ppermute | solution.py:18
  496.9 8.7 %collective-permute-start.2 = (f32[128,97]{1,0:T(8,128)S(1)}, f32[128,97]{1,0:T(8,128)S(1)}, u32[]{:S(2)}, u32[]{:S(2)}) collective-permute-start(f32[128,97]{1,0:T(8,128)S(1)} %get-tuple-element.367), channel_id=1, source_target_pairs={{0,16},{16,32},{32,48},{1,17},{17,33},{33,49},{2,18},{18,34},{34,5... | collective-permute-start | bytes 149000 | tf_op jit(solution)/shard_map/ppermute | solution.py:18
  504.3 7.8 %collective-permute-start.3 = (f32[128,97]{1,0:T(8,128)S(1)}, f32[128,97]{1,0:T(8,128)S(1)}, u32[]{:S(2)}, u32[]{:S(2)}) collective-permute-start(f32[128,97]{1,0:T(8,128)S(1)} %get-tuple-element.366), channel_id=1, source_target_pairs={{16,0},{32,16},{48,32},{17,1},{33,17},{49,33},{18,2},{34,18},{50,3... | collective-permute-start | bytes 149000 | tf_op jit(solution)/shard_map/ppermute | solution.py:18
where the time goes:
time: 587 us; the launch traced here: 579 us
  local copies, waits for them, and re-layouts  205 us (35%)
  loops' own time  160 us (27%)
  matrix products  118 us (20%)
  blocking collectives  64.2 us (11%)
  starting transfers between devices  14.1 us (2%)
  waiting for transfers between devices  11.8 us (2%)
  other arithmetic  5.88 us (1%)
    another operation x1, loops' own time, shards(): screen = lax.fori_loop(0, slices, march_slab, screen)  160 us
    dot_general x48, matrix products, march_slab(): jnp.dot(slab, placing, precision=lax.Precision.HIGHEST, preferred_element...  118 us
    dynamic_update_slice x48, local copies, waits for them, and re-layouts, march_slab(): lax.dynamic_update_slice(carry, window + spread, (start_u, jnp.int32(0)))  73.2 us
    pmax x5, blocking collectives, one_axis_at_a_time(): return functools.reduce(lax.pmax, axes, array)  50.1 us
    dynamic_slice x48, local copies, waits for them, and re-layouts, march_slab(): lax.dynamic_index_in_dim(shear_fractions, slice_index, 1, keepdims=False)  36.3 us
    dynamic_slice x48, local copies, waits for them, and re-layouts, march_slab(): lax.dynamic_index_in_dim(shear_offsets, slice_index, 1, keepdims=False)  36.2 us
    slice x48, local copies, waits for them, and re-layouts, march_slab(): start_u = offset_pair[0] - center + margin  28.6 us
    slice x48, local copies, waits for them, and re-layouts, march_slab(): frac_u = frac_pair[0]  28 us
  transfers between devices with their start and end apart: 4, of which 3 were waited for; matrix products, arithmetic and copies ran while one was open for 0% of the time, Pallas kernels for 0%

commit v1 on v0

v1 whole, which is shorter than its diff:
```python
import functools

import jax
import jax.numpy as jnp
from jax import lax
from jax.experimental import pallas as pl
from jax.experimental.pallas import tpu as pltpu
from jax.sharding import PartitionSpec as P

MESH = pl.DeviceIdType.MESH
ROWS = 8
LANES = 128
CHUNKS = 4


def remote(src, dst, send_sem, recv_sem, device_id):
    return pltpu.make_async_remote_copy(
        src_ref=src, dst_ref=dst, send_sem=send_sem, recv_sem=recv_sem, device_id=device_id, device_id_type=MESH
    )


def march(bufs, offs, fracs, lane, chunk, accs):
    per = bufs[0].shape[0]
    base_u = offs[0, 0]
    base_v = offs[1, 0]
    pad = (bufs[0].shape[1] - LANES) // 2
    vregs = len(accs) // 2
    buf = bufs[chunk]

    def one(local, accs):
        z = chunk * per + local
        su = offs[0, z] - base_u
        sv = offs[1, z] - base_v
        fu = fracs[0, z]
        fv = fracs[1, z]
        gu = 1.0 - fu
        gv = 1.0 - fv
        early = lane < sv
        early1 = lane <= sv
        wa0 = jnp.where(early, 0.0, gv)
        wb0 = jnp.where(early, gv, 0.0)
        wa1 = jnp.where(early1, 0.0, fv)
        wb1 = jnp.where(early1, fv, 0.0)
        out = []
        for j in range(vregs):
            here = buf[local, pl.ds(ROWS * j + pad - su, ROWS), :]
            before = buf[local, pl.ds(ROWS * j + pad - 1 - su, ROWS), :]
            q = here * gu + before * fu
            r0 = pltpu.roll(q, sv, 1)
            r1 = pltpu.roll(r0, 1, 1)
            out.append(accs[2 * j] + (r0 * wa0 + r1 * wa1))
            out.append(accs[2 * j + 1] + (r0 * wb0 + r1 * wb1))
        return tuple(out)

    return lax.fori_loop(0, per, one, accs)


def kernel(
    sizes, offs, fracs, flat, density, out,
    buf0, buf1, buf2, buf3, win, frame, summed, got_pair, got_y, red, got_halo, peak, got_m1, peak2, got_m2,
    sem_in, s_pair, r_pair, s_y, r_y, s_halo, r_halo, s_m1, r_m1, s_m2, r_m2,
):
    nx, ny, nz = sizes
    chips = nz // 2
    bufs = (buf0, buf1, buf2, buf3)
    per = buf0.shape[0]
    pad = (buf0.shape[1] - LANES) // 2
    gx = lax.axis_index("gx")
    gy = lax.axis_index("gy")
    gz = lax.axis_index("gz")
    chip = gz // 2
    core = gz % 2
    plane = gx * ny + gy

    loads = [
        pltpu.make_async_copy(
            density.at[pl.ds(c * per, per)], bufs[c].at[:, pl.ds(pad, LANES), :], sem_in.at[c]
        )
        for c in range(CHUNKS)
    ]
    for load in loads:
        load.start()

    barrier = pltpu.get_barrier_semaphore()

    def greet_z(d, carry):
        pl.semaphore_signal(barrier, inc=1, device_id={"gz": (gz + d) % nz}, device_id_type=MESH)
        return carry

    def greet_plane(d, carry):
        other = (plane + d) % (nx * ny)
        pl.semaphore_signal(
            barrier, inc=1, device_id={"gx": other // ny, "gy": other % ny}, device_id_type=MESH
        )
        return carry

    lax.fori_loop(1, nz, greet_z, 0)
    lax.fori_loop(1, nx * ny, greet_plane, 0)

    zero = jnp.zeros((ROWS, LANES), jnp.float32)
    edge = jnp.zeros((pad, LANES), jnp.float32)
    for c in range(CHUNKS):
        for local in range(per):
            bufs[c][local, pl.ds(0, pad), :] = edge
            bufs[c][local, pl.ds(pad + LANES, pad), :] = edge
    vregs = (LANES + pad) // ROWS
    top = 192
    total = win.shape[1]
    for half in range(2):
        win[half, pl.ds(0, top), :] = jnp.zeros((top, LANES), jnp.float32)
        rest = total - top - vregs * ROWS
        win[half, pl.ds(top + vregs * ROWS, rest), :] = jnp.zeros((rest, LANES), jnp.float32)

    lane = lax.broadcasted_iota(jnp.int32, (ROWS, LANES), 1)
    accs = (zero,) * (2 * vregs)
    for c in range(CHUNKS):
        loads[c].wait()
        accs = march(bufs, offs, fracs, lane, c, accs)
    for j in range(vregs):
        for half in range(2):
            win[half, pl.ds(top + ROWS * j, ROWS), :] = accs[2 * j + half]

    blocks = LANES // ROWS
    base_u = offs[0, 0]
    shift = offs[1, 0] + 32
    wide = shift >= LANES
    turn = jnp.where(wide, shift - LANES, shift)
    first = lane < turn
    far = jnp.full((ROWS, LANES), shift, jnp.int32) >= LANES
    for j in range(3 * blocks):
        tu, rb = j // blocks, j % blocks
        if ROWS * j < 32 or ROWS * j > 32 + 192 + LANES:
            tiles = (zero, zero, zero)
        else:
            start = ROWS * j - 32 + top - base_u
            ra = pltpu.roll(win[0, pl.ds(start, ROWS), :], turn, 1)
            rb_ = pltpu.roll(win[1, pl.ds(start, ROWS), :], turn, 1)
            x0 = jnp.where(first, 0.0, ra)
            x1 = jnp.where(first, ra, rb_)
            x2 = jnp.where(first, rb_, 0.0)
            tiles = (jnp.where(far, 0.0, x0), jnp.where(far, x0, x1), jnp.where(far, x1, x2))
        for tv in range(3):
            frame[rb % 2, rb // 2, 3 * tu + tv] = tiles[tv]

    pl.semaphore_wait(barrier, nz - 1 + nx * ny - 1)

    swap = remote(frame.at[1 - core], got_pair, s_pair, r_pair, {"gz": chip * 2 + 1 - core})
    swap.start()
    swap.wait_recv()

    def y_copy(d):
        to = (chip + d) % chips
        return to, remote(
            summed.at[to], got_y.at[d], s_y.at[d], r_y.at[d], {"gz": to * 2 + core}
        )

    order = sorted(range(1, chips), key=lambda d: -min(d, chips - d))
    sends = []
    for d in order:
        to, copy = y_copy(d)
        summed[to] = frame[core, to] + got_pair[to]
        copy.start()
        sends.append(copy)
    mine = frame[core, chip] + got_pair[chip]
    for d in reversed(order):
        y_copy(d)[1].wait_recv()
        mine = mine + got_y[d]
    red[...] = mine

    steps = [(tu, tv) for tu in (0, 2) for tv in (0, 2)] + [(0, 1), (2, 1), (1, 0), (1, 2)]

    def inside(u, v):
        return (u >= 0) & (u < nx) & (v >= 0) & (v < ny)

    def halo(tu, tv):
        t = 3 * tu + tv
        return remote(
            red.at[t], got_halo.at[t], s_halo.at[t], r_halo.at[t], {"gx": gx + tu - 1, "gy": gy + tv - 1}
        )

    for tu, tv in steps:
        @pl.when(inside(gx + tu - 1, gy + tv - 1))
        def _():
            halo(tu, tv).start()

        @pl.when(jnp.logical_not(inside(gx - tu + 1, gy - tv + 1)))
        def _():
            got_halo[3 * tu + tv] = zero

    integral = mine[4]
    for tu, tv in reversed(steps):
        @pl.when(inside(gx - tu + 1, gy - tv + 1))
        def _():
            halo(tu, tv).wait_recv()

        integral = integral + got_halo[3 * tu + tv]

    detected = flat[...] * jnp.exp(-integral)
    top_row = jnp.max(detected, axis=0, keepdims=True)
    peak[0] = top_row

    def m1_copy(d):
        return remote(peak, got_m1.at[d], s_m1.at[d], r_m1.at[d], {"gz": (gz + d) % nz})

    def m2_copy(d):
        other = (plane + d) % (nx * ny)
        return remote(
            peak2, got_m2.at[d], s_m2.at[d], r_m2.at[d], {"gx": other // ny, "gy": other % ny}
        )

    def spread(copy_of, count):
        def go(d, carry):
            copy_of(d).start()
            return carry

        lax.fori_loop(1, count, go, 0)

    def collect(copy_of, got, count, largest):
        def take(d, largest):
            copy_of(d).wait_recv()
            return jnp.maximum(largest, got[d, 0])

        return lax.fori_loop(1, count, take, largest)

    spread(m1_copy, nz)
    largest = collect(m1_copy, got_m1, nz, top_row)
    peak2[0] = largest
    spread(m2_copy, nx * ny)
    largest = collect(m2_copy, got_m2, nx * ny, largest)
    out[...] = detected / jnp.max(largest)

    swap.wait_send()
    for copy in sends:
        copy.wait_send()
    for tu, tv in steps:
        @pl.when(inside(gx + tu - 1, gy + tv - 1))
        def _():
            halo(tu, tv).wait_send()

    def sent(copy_of, count):
        def done(d, carry):
            copy_of(d).wait_send()
            return carry

        lax.fori_loop(1, count, done, 0)

    sent(m1_copy, nz)
    sent(m2_copy, nx * ny)


def shards(sizes, density, shear_offsets, shear_fractions, flat_field):
    nx, ny, nz = sizes
    slices = density.shape[0]
    chips = nz // 2
    pad = slices
    vmem = pltpu.VMEM
    dma = pltpu.SemaphoreType.DMA
    f32 = jnp.float32
    smem = pl.BlockSpec(memory_space=pltpu.SMEM)
    invmem = pl.BlockSpec(memory_space=pltpu.VMEM)
    return pl.pallas_call(
        functools.partial(kernel, sizes),
        out_shape=jax.ShapeDtypeStruct(flat_field.shape, f32),
        in_specs=[smem, smem, invmem, pl.BlockSpec(memory_space=pl.ANY)],
        out_specs=invmem,
        scratch_shapes=[vmem((slices // CHUNKS, LANES + 2 * pad, LANES), f32) for _ in range(CHUNKS)]
        + [
            vmem((2, 528, LANES), f32),
            vmem((2, chips, 9, ROWS, LANES), f32),
            vmem((chips, 9, ROWS, LANES), f32),
            vmem((chips, 9, ROWS, LANES), f32),
            vmem((chips, 9, ROWS, LANES), f32),
            vmem((9, ROWS, LANES), f32),
            vmem((9, ROWS, LANES), f32),
            vmem((1, 1, LANES), f32),
            vmem((nz, 1, 1, LANES), f32),
            vmem((1, 1, LANES), f32),
            vmem((nx * ny, 1, 1, LANES), f32),
            dma((CHUNKS,)),
            dma, dma,
            dma((chips,)), dma((chips,)),
            dma((9,)), dma((9,)),
            dma((nz,)), dma((nz,)),
            dma((nx * ny,)), dma((nx * ny,)),
        ],
        compiler_params=pltpu.CompilerParams(collective_id=0, has_side_effects=True),
    )(shear_offsets, shear_fractions, flat_field, density)


def solution(mesh):
    sizes = (mesh.shape["gx"], mesh.shape["gy"], mesh.shape["gz"])
    return jax.shard_map(
        functools.partial(shards, sizes),
        mesh=mesh,
        in_specs=(P("gz", "gx", "gy"), P(None, "gz"), P(None, "gz"), P(("gx", "gz"), "gy")),
        out_specs=P(("gx", "gz"), "gy"),
        check_vma=False,
    )
```

time: 587 us -> 50.5 us (0.09); the launches traced: 579 us -> 50.3 us
  local copies, waits for them, and re-layouts: 205 us -> 1.28 us
  loops' own time: 160 us -> 0 us
  matrix products: 118 us -> 0 us
  blocking collectives: 64.2 us -> 0 us
  Pallas kernels: 0 us -> 49 us
  starting transfers between devices: 14.1 us -> 0 us
  waiting for transfers between devices: 11.8 us -> 0 us
  other arithmetic: 5.88 us -> 0 us
    another operation x1 -> x0, loops' own time: 160 us -> none  [shards(): screen = lax.fori_loop(0, slices, march_slab, screen)]
    dot_general x48 -> x0, matrix products: 118 us -> none  [march_slab(): jnp.dot(slab, placing, precision=lax.Precision.HIGHEST, preferred_element...]
    dynamic_update_slice x48 -> x0, local copies, waits for them, and re-layouts: 73.2 us -> none  [march_slab(): lax.dynamic_update_slice(carry, window + spread, (start_u, jnp.int32(0)))]
    dynamic_slice x96 -> x0, local copies, waits for them, and re-layouts: 72.5 us -> none  [the longest x48 36.3 us: march_slab(): lax.dynamic_index_in_dim(shear_fractions, slice_index, 1, keepdims=False)]
    slice x100 -> x0, local copies, waits for them, and re-layouts: 56.8 us -> none  [the longest x48 28.6 us: march_slab(): start_u = offset_pair[0] - center + margin]
    pmax x5 -> x0, blocking collectives: 50.1 us -> none  [one_axis_at_a_time(): return functools.reduce(lax.pmax, axes, array)]
    pallas_call x0 -> x1, Pallas kernels: none -> 49 us  [shards(): pl.pallas_call(functools.partial(kernel, sizes), out_shape=jax.ShapeDtype...]
    all_to_all x1 -> x0, blocking collectives: 14.1 us -> none  [sum_at_owner(): tiles = lax.all_to_all(in_blocks(array, dim, size), axis, 0, 0, tiled=True)]
  transfers between devices with their start and end apart: 4 -> 0, of which waited for: 3 -> 0; matrix products, arithmetic and copies ran while one was open for 0% -> 0% of each run, Pallas kernels for 0% -> 0%
where the time goes in v1:
time: 50.5 us; the launch traced here: 50.3 us
  Pallas kernels  49 us (97%)
  local copies, waits for them, and re-layouts  1.28 us (3%)
    pallas_call x1, Pallas kernels, shards(): pl.pallas_call(functools.partial(kernel, sizes), out_shape=jax.ShapeDtype...  49 us
    unnamed x1, local copies, waits for them, and re-layouts  1.28 us

profile of v1, /device:TPU:1, one launch (start us, length us, event | category | flops | bytes accessed | tf_op | source)
XLA Modules:
  0.0 50.3 jit_solution(16619137544031284345)
XLA Ops:
  0.0 49.0 %shard_map.46 = f32[8,128]{1,0:T(8,128)} custom-call(s32[2,48]{1,0:T(2,128)} %offs.1, f32[2,48]{1,0:T(2,128)} %fracs.1, f32[8,128]{1,0:T(8,128)} %flat.1, f32[48,128,128]{2,1,0:T(8,128)} %density.1), custom_call_target="tpu_custom_call" | custom-call | tf_op jit(solution)/shard_map/pallas_call | solution.py:261
  49.0 1.3 %copy.6 = f32[8,128]{1,0:T(8,128)} copy(f32[8,128]{1,0:T(8,128)} %shard_map.46) | data formatting | bytes 8192
